TPU v7x, 32 devices: a whole 2x2x4 slice. The times are simulated.
32 devices in a mesh: samp: 4 (over z), atom: 8 (over y, x, core).
Axes of the slice: x: 2, y: 2, z: 4, core: 2. Of those that a mesh axis runs over, the one named last changes fastest.
Arguments:
- atom_state: bfloat16 [16, 2560, 128], P('samp', 'atom'), may hold values from -6 to 6, as said below
- atom_token: int32 [2560], P('atom'), may hold values from 0 to 319, never falling along the last dimension, each value on 1 to 24 neighbouring positions
- window_valid: int32 [80], P('atom'), may hold values from 1 to 32
- attend_gain: float32 [128], replicated, may hold values from 0.25 to 1.75
- project_weight: bfloat16 [128, 384], replicated, may hold values from -4 to 4
- output_weight: bfloat16 [128, 128], replicated, may hold values from -1.5 to 1.5
- token_bias: float32 [4], replicated, may hold values from -2 to 2
- transit_gain: float32 [128], replicated, may hold values from 0.25 to 1.75
- transit_weight: bfloat16 [128, 512], replicated, may hold values from -0.5 to 0.5
- return_weight: bfloat16 [256, 128], replicated, may hold values from -0.375 to 0.375
- cotangent: bfloat16 [16, 2560, 128], P('samp', 'atom'), may hold values from -6 to 6
Outputs:
- block_out: bfloat16 [16, 2560, 128], P('samp', 'atom')
- state_grad: bfloat16 [16, 2560, 128], P('samp', 'atom')
- grad_attend_gain: float32 [128], replicated
- grad_project: float32 [128, 384], replicated
- grad_output: float32 [128, 128], replicated
- grad_bias: float32 [4], replicated
- grad_transit_gain: float32 [128], replicated
- grad_transit: float32 [128, 512], replicated
- grad_return: float32 [256, 128], replicated
Inputs may be any that keep to these rules, and one draw needn't show every extreme that they name: atom_state is finite. `atom_token`: tokens are numbered in order along the atoms; a token has 1 to 24 atoms.
All inputs are finite; a program needn't handle non-finite values.
Results may differ from a plain program's by a relative error of at most 0.025.
The roundings to bfloat16 on the way count: a program that leaves them out, or rounds other values in their place, can miss the bound.
Values may be sent and summed in bfloat16 or wider, within the bound.
No kernel may reach another device: no remote copies, remote signals or barrier semaphores. Data moves between devices by JAX's collectives and lax.ppermute only.
A program may use at most 64 MiB of HBM per device.

v0:
```python
import jax
import jax.numpy as jnp
from jax import lax
from jax.sharding import PartitionSpec as P

HEADS = 4
TRANS = 256
QWIN = 32
KWIN = 128
HALO = 48
PRECISE = lax.Precision.HIGHEST
EPSILON = 1e-05
CLIP_NORM = 256.0


def with_halo(value, sides, width):
    for axis, dim in sides:
        size, length = (lax.axis_size(axis), value.shape[dim])
        up = [(i, (i + 1) % size) for i in range(size - 1)]
        down = [(j, i) for i, j in up]
        last = lax.slice_in_dim(value, length - width, length, axis=dim)
        first = lax.slice_in_dim(value, 0, width, axis=dim)
        before = lax.ppermute(last, axis, up)
        after = lax.ppermute(first, axis, down)
        value = jnp.concatenate([before, value, after], axis=dim)
    return value


def passed_along(value, axis, by):
    size = lax.axis_size(axis)
    pairs = [(i, i + by) for i in range(size) if 0 <= i + by < size]
    return lax.ppermute(value, axis, pairs)


def normalize(values, scaling):
    values = values.astype(jnp.float32)
    center = jnp.mean(values, axis=-1, keepdims=True)
    shifted = values - center
    variance = jnp.mean(shifted * shifted, axis=-1, keepdims=True)
    return shifted * lax.rsqrt(variance + EPSILON) * scaling


def token_codes(atom_token, window_valid):
    windows_here = window_valid.shape[0]
    slots = lax.broadcasted_iota(jnp.int32, (windows_here, QWIN), 1)
    inside = (slots < window_valid[:, None]).reshape(-1)
    return jnp.where(inside, atom_token + 1, 0)


def attend(queries, pairs, query_ids, ext_ids, token_bias):
    channels = queries.shape[1]
    window_count = queries.shape[0] // QWIN
    extra_blocks = 2 * HALO // QWIN
    span_blocks = KWIN // QWIN
    head_dim = channels // HEADS
    blocks = pairs.reshape(window_count + extra_blocks, QWIN, 2 * channels)
    gathered = jnp.concatenate(
        [blocks[offset : offset + window_count] for offset in range(span_blocks)], axis=1
    )
    code_blocks = ext_ids.reshape(window_count + extra_blocks, QWIN)
    key_ids = jnp.concatenate(
        [code_blocks[offset : offset + window_count] for offset in range(span_blocks)], axis=1
    )
    query_blocks = queries.reshape(window_count, QWIN, HEADS, head_dim)
    keys_in = gathered[:, :, :channels].reshape(window_count, KWIN, HEADS, head_dim)
    values_in = gathered[:, :, channels:].reshape(window_count, KWIN, HEADS, head_dim)
    scores = jnp.einsum("wqhd,wkhd->whqk", query_blocks, keys_in, precision=PRECISE) / jnp.sqrt(
        float(head_dim)
    )
    query_codes = query_ids.reshape(window_count, QWIN)
    same_token = (query_codes[:, :, None] == key_ids[:, None, :]).astype(jnp.float32)
    scores = scores + token_bias[None, :, None, None] * same_token[:, None, :, :]
    usable_key = (key_ids > 0)[:, None, None, :]
    scores = jnp.where(usable_key, scores, -1e30)
    highest = lax.stop_gradient(jnp.max(scores, axis=-1, keepdims=True))
    weights = jnp.exp(scores - highest)
    weights = weights / jnp.sum(weights, axis=-1, keepdims=True)
    outcome = jnp.einsum("whqk,wkhd->wqhd", weights, values_in, precision=PRECISE)
    return outcome.reshape(window_count * QWIN, channels)


def place_rims(center, from_before, from_after):
    atoms_here = center.shape[1]
    lower = jnp.pad(from_before, ((0, 0), (0, atoms_here - HALO), (0, 0)))
    upper = jnp.pad(from_after, ((0, 0), (atoms_here - HALO, 0), (0, 0)))
    return center + lower + upper


def on_device(
    atom_state,
    atom_token,
    window_valid,
    attend_gain,
    project_weight,
    output_weight,
    token_bias,
    transit_gain,
    transit_weight,
    return_weight,
    cotangent,
):
    channels = atom_state.shape[2]
    atoms_here = atom_state.shape[1]
    query_ids = token_codes(atom_token, window_valid)
    ext_ids = with_halo(query_ids, (("atom", 0),), HALO)
    normed = normalize(atom_state, attend_gain).astype(jnp.bfloat16)
    query_part = project_weight[:, :channels]
    pair_part = project_weight[:, channels:]
    ext_normed = with_halo(normed, (("atom", 1),), HALO)
    queries = jnp.dot(normed, query_part, preferred_element_type=jnp.float32).astype(jnp.bfloat16)
    ext_pairs = jnp.dot(ext_normed, pair_part, preferred_element_type=jnp.float32).astype(
        jnp.bfloat16
    )

    def forward_one(operands):
        query_rows, pair_rows = operands
        return attend(
            query_rows.astype(jnp.float32),
            pair_rows.astype(jnp.float32),
            query_ids,
            ext_ids,
            token_bias,
        )

    attended = lax.map(forward_one, (queries, ext_pairs)).astype(jnp.bfloat16)
    residual = (
        atom_state.astype(jnp.float32)
        + jnp.dot(attended, output_weight, preferred_element_type=jnp.float32)
    ).astype(jnp.bfloat16)
    transit_in = normalize(residual, transit_gain).astype(jnp.bfloat16)
    both_parts = jnp.dot(transit_in, transit_weight, preferred_element_type=jnp.float32)
    gate_part = both_parts[:, :, :TRANS]
    up_part = both_parts[:, :, TRANS:]
    gated = (jax.nn.silu(gate_part) * up_part).astype(jnp.bfloat16)
    block_out = (
        residual.astype(jnp.float32)
        + jnp.dot(gated, return_weight, preferred_element_type=jnp.float32)
    ).astype(jnp.bfloat16)
    grad_return = jnp.einsum("sai,sac->ic", gated, cotangent, preferred_element_type=jnp.float32)
    back_gated = jnp.einsum(
        "sac,ic->sai", cotangent, return_weight, preferred_element_type=jnp.float32
    )
    sigmoid_gate = jax.nn.sigmoid(gate_part)
    back_gate = back_gated * up_part * sigmoid_gate * (1.0 + gate_part * (1.0 - sigmoid_gate))
    back_up = back_gated * gate_part * sigmoid_gate
    back_hidden = jnp.concatenate([back_gate, back_up], axis=-1).astype(jnp.bfloat16)
    grad_transit = jnp.einsum(
        "sac,sae->ce", transit_in, back_hidden, preferred_element_type=jnp.float32
    )
    back_transit = jnp.einsum(
        "sae,ce->sac", back_hidden, transit_weight, preferred_element_type=jnp.float32
    )
    _, pull_second = jax.vjp(normalize, residual.astype(jnp.float32), transit_gain)
    back_res_norm, grad_transit_gain = pull_second(back_transit)
    back_residual = cotangent.astype(jnp.float32) + back_res_norm
    back_res16 = back_residual.astype(jnp.bfloat16)
    grad_output = jnp.einsum(
        "sac,sae->ce", attended, back_res16, preferred_element_type=jnp.float32
    )
    back_attended = jnp.einsum(
        "sae,ce->sac", back_res16, output_weight, preferred_element_type=jnp.float32
    )

    def backward_one(operands):
        query_rows, pair_rows, back_rows = operands

        def local_attend(query_in, pairs_in, bias_in):
            return attend(query_in, pairs_in, query_ids, ext_ids, bias_in)

        _, pull_attend = jax.vjp(
            local_attend, query_rows.astype(jnp.float32), pair_rows.astype(jnp.float32), token_bias
        )
        return pull_attend(back_rows)

    back_queries, back_ext, bias_parts = lax.map(backward_one, (queries, ext_pairs, back_attended))
    grad_bias = jnp.sum(bias_parts, axis=0)
    grad_query = jnp.einsum(
        "sac,sae->ce", normed.astype(jnp.float32), back_queries, precision=PRECISE
    )
    grad_pairs = jnp.einsum(
        "sac,sae->ce", ext_normed.astype(jnp.float32), back_ext, precision=PRECISE
    )
    grad_project = jnp.concatenate([grad_query, grad_pairs], axis=1)
    back_ext_normed = jnp.einsum(
        "sae,ce->sac", back_ext, pair_part.astype(jnp.float32), precision=PRECISE
    )
    from_before = passed_along(
        back_ext_normed[:, HALO + atoms_here :].astype(jnp.bfloat16), "atom", 1
    ).astype(jnp.float32)
    from_after = passed_along(back_ext_normed[:, :HALO].astype(jnp.bfloat16), "atom", -1).astype(
        jnp.float32
    )
    own_rows = back_ext_normed[:, HALO : HALO + atoms_here] + jnp.einsum(
        "sae,ce->sac", back_queries, query_part.astype(jnp.float32), precision=PRECISE
    )
    back_normed = place_rims(own_rows, from_before, from_after)
    _, pull_first = jax.vjp(normalize, atom_state.astype(jnp.float32), attend_gain)
    back_state_norm, grad_attend_gain = pull_first(back_normed)
    state_grad = (back_residual + back_state_norm).astype(jnp.bfloat16)
    gradients = (
        grad_attend_gain,
        grad_project,
        grad_output,
        grad_bias,
        grad_transit_gain,
        grad_transit,
        grad_return,
    )
    totals = lax.psum(
        (
            gradients[0],
            gradients[1],
            gradients[2],
            gradients[3],
            gradients[4],
            gradients[5],
            gradients[6],
        ),
        ("samp", "atom"),
    )
    squares = sum((jnp.sum(member * member) for member in totals))
    factor = CLIP_NORM / jnp.sqrt(squares + CLIP_NORM * CLIP_NORM)
    clipped = tuple((member * factor for member in totals))
    return (
        block_out,
        state_grad,
        clipped[0],
        clipped[1],
        clipped[2],
        clipped[3],
        clipped[4],
        clipped[5],
        clipped[6],
    )


def solution(mesh):
    return jax.shard_map(
        on_device,
        mesh=mesh,
        in_specs=(
            P("samp", "atom", None),
            P("atom"),
            P("atom"),
            P(),
            P(),
            P(),
            P(),
            P(),
            P(),
            P(),
            P("samp", "atom", None),
        ),
        out_specs=(
            P("samp", "atom", None),
            P("samp", "atom", None),
            P(),
            P(),
            P(),
            P(),
            P(),
            P(),
            P(),
        ),
        check_vma=False,
    )
```

profile of v0, /device:TPU:0, one launch (start us, length us, event | category | flops | bytes accessed | tf_op | source)
XLA Modules:
  0.0 380.1 jit_solution(13928921964016010154)
XLA Ops:
  8.9 2.4 collective-permute-start.2
  16.6 5.1 %collective-permute-start = (bf16[4,48,128]{2,1,0:T(8,128)(2,1)S(1)}, bf16[4,48,128]{2,1,0:T(8,128)(2,1)S(1)}, u32[]{:S(2)}, u32[]{:S(2)}) collective-permute-start(bf16[4,48,128]{2,1,0:T(8,128)(2,1)S(1)} %get-tuple-element.304), channel_id=1, source_target_pairs={{0,1},{1,2},{2,3},{3,4},{4,5},{5,6},{6,7},{8,9},{9,10},{10,11},{11... | collective-permute-start | bytes 147464 | tf_op jit(solution)/shard_map/ppermute | solution.py:23
  27.4 67.5 %while.30 = (s32[]{:T(128)}, bf16[4,320,128]{2,1,0:T(8,128)(2,1)}, bf16[4,416,256]{2,1,0:T(8,128)(2,1)}, s32[10,1,1,128]{3,0,2,1:T(8,128)S(1)}, bf16[4,320,128]{...) while((s32[]{:T(128)}, bf16[4,320,128]{2,1,0:T(8,128)(2,1)}, ...), condition=%wide.region_5.6_spmd.clone, body=%wide.region_2.5_spmd.sunk.clone | while | flops 128473856 | bytes 16410097 | solution.py:125
  33.0 2.4 copy.101
  36.9 2.8 pad_maximum_fusion.13
  49.9 2.4 copy.101
  53.8 2.8 pad_maximum_fusion.13
  66.7 2.4 copy.101
  70.7 2.8 pad_maximum_fusion.13
  83.6 2.4 copy.101
  87.5 2.8 pad_maximum_fusion.13
  106.7 102.9 %while.31 = (s32[]{:T(128)}, f32[4,320,128]{2,1,0:T(8,128)}, f32[4,416,256]{2,1,0:T(8,128)}, f32[4,4]{1,0:T(4,128)S(1)}, s32[10,1,1,128]{3,0,2,1:T(8,128)S(1)}, ...) while((s32[]{:T(128)}, f32[4,320,128]{2,1,0:T(8,128)}, ...), condition=%wide.region_15.16_spmd.clone, body=%wide.region_10.15_spmd.sunk.clone | while | flops 319997184 | bytes 31044328 | solution.py:175
  114.3 2.4 copy.108
  116.7 2.4 copy.109
  119.2 2.8 pad_maximum_fusion.14
  139.9 2.4 copy.108
  142.4 2.4 copy.109
  144.8 2.8 pad_maximum_fusion.14
  165.6 2.4 copy.108
  168.1 2.4 copy.109
  170.5 2.8 pad_maximum_fusion.14
  191.3 2.4 copy.108
  193.7 2.4 copy.109
  196.2 2.8 pad_maximum_fusion.14
  209.6 2.5 fusion.84
  212.7 4.7 %collective-permute-start.4 = (bf16[4,48,128]{2,1,0:T(8,128)(2,1)S(1)}, bf16[4,48,128]{2,1,0:T(8,128)(2,1)S(1)}, u32[]{:S(2)}, u32[]{:S(2)}) collective-permute-start(bf16[4,48,128]{2,1,0:T(8,128)(2,1)S(1)} %get-tuple-element.302), channel_id=1, source_target_pairs={{0,1},{1,2},{2,3},{3,4},{4,5},{5,6},{6,7},{8,9},{9,10},{10,11},{11... | collective-permute-start | bytes 147464 | tf_op jit(solution)/shard_map/ppermute | solution.py:32
  221.2 1.8 fusion.42
  223.9 44.4 %all-reduce.8 = (f32[128]{0:T(128)S(1)}, f32[4]{0:T(128)S(1)}, f32[128]{0:T(128)S(1)}) all-reduce(f32[128]{0:T(128)S(1)} %get-tuple-element.226, f32[4]{0:T(128)S(1)} %reduce_sum.232, f32[128]{0:T(128)S(1)} %copy-done.29), channel_id=1, replica_groups=mesh['samp'=4,'atom'=8] {'samp','atom'}, use_global_device_ids=true, to_apply=%region_19.20 | all-reduce | flops 260 | bytes 2080 | tf_op jit(solution)/shard_map/psum | solution.py:209
  270.2 1.7 add_convert_fusion
  271.9 84.5 %all-reduce.12.cloned.1.call-done = (f32[128,384]{1,0:T(8,128)}, f32[128,128]{1,0:T(8,128)}, f32[128,512]{1,0:T(8,128)}, f32[256,128]{1,0:T(8,128)}) async-done(((f32[128,384]{1,0:T(8,128)}, f32[128,128]{1,0:T(8,128)}, f32[128,512]{1,0:T(8,128)}, f32[256,128]{1,0:T(8,128)}), (f32[128,384]{1,0:T(8,128)}, f32[128,128]{1,0:T(8,128)}, f32[128,512]{1,0:T(8,128)}, ...) | async-done | bytes 655376 | tf_op jit(solution)/shard_map/psum | solution.py:209
  358.0 1.6 multiply_reduce_fusion.5
  369.2 1.7 broadcast_multiply_fusion
  (341 shorter events, 158.1 us)
Async XLA Ops:
  7.2 89.7 %copy-start = (bf16[128,512]{1,0:T(8,128)(2,1)S(1)}, bf16[128,512]{1,0:T(8,128)(2,1)}, u32[]{:S(2)}) copy-start(bf16[128,512]{1,0:T(8,128)(2,1)} %param.23) | copy-start | bytes 393220
  7.2 16.6 %copy-start.15 = (bf16[128,384]{1,0:T(8,128)(2,1)S(1)}, bf16[128,384]{1,0:T(8,128)(2,1)}, u32[]{:S(2)}) copy-start(bf16[128,384]{1,0:T(8,128)(2,1)} %param.19) | copy-start | bytes 294916
  7.2 349.2 %all-reduce.12.cloned.1.call-start = ((), (), s32[]{:S(2)}) async-start(), calls=%async_computation | async-start | bytes 1310720 | tf_op jit(solution)/shard_map/psum | solution.py:209
  8.9 15.9 %collective-permute-start.2 = (s32[48]{0:T(128)S(1)}, s32[48]{0:T(128)S(1)}, u32[]{:S(2)}, u32[]{:S(2)}) collective-permute-start(s32[48]{0:T(128)S(1)} %get-tuple-element.310), channel_id=1, source_target_pairs={{0,1},{1,2},{2,3},{3,4},{4,5},{5,6},{6,7},{8,9},{9,10},{10,11},{11... | collective-permute-start | bytes 584 | tf_op jit(solution)/shard_map/ppermute | solution.py:23
  11.3 13.5 %collective-permute-start.3 = (s32[48]{0:T(128)S(1)}, s32[48]{0:T(128)S(1)}, u32[]{:S(2)}, u32[]{:S(2)}) collective-permute-start(s32[48]{0:T(128)S(1)} %get-tuple-element.311), channel_id=1, source_target_pairs={{1,0},{2,1},{3,2},{4,3},{5,4},{6,5},{7,6},{9,8},{10,9},{11,10},{12... | collective-permute-start | bytes 584 | tf_op jit(solution)/shard_map/ppermute | solution.py:24
  16.6 10.8 %copy-start.5 = (bf16[4,320,128]{2,1,0:T(8,128)(2,1)}, bf16[4,320,128]{2,1,0:T(8,128)(2,1)S(1)}, u32[]{:S(2)}) copy-start(bf16[4,320,128]{2,1,0:T(8,128)(2,1)S(1)} %fusion.39) | copy-start | bytes 983044
  16.6 9.1 %collective-permute-start = (bf16[4,48,128]{2,1,0:T(8,128)(2,1)S(1)}, bf16[4,48,128]{2,1,0:T(8,128)(2,1)S(1)}, u32[]{:S(2)}, u32[]{:S(2)}) collective-permute-start(bf16[4,48,128]{2,1,0:T(8,128)(2,1)S(1)} %get-tuple-element.304), channel_id=1, source_target_pairs={{0,1},{1,2},{2,3},{3,4},{4,5},{5,6},{6,7},{8,9},{9,10},{10,11},{11... | collective-permute-start | bytes 147464 | tf_op jit(solution)/shard_map/ppermute | solution.py:23
  21.7 4.4 %collective-permute-start.1 = (bf16[4,48,128]{2,1,0:T(8,128)(2,1)S(1)}, bf16[4,48,128]{2,1,0:T(8,128)(2,1)S(1)}, u32[]{:S(2)}, u32[]{:S(2)}) collective-permute-start(bf16[4,48,128]{2,1,0:T(8,128)(2,1)S(1)} %get-tuple-element.305), channel_id=1, source_target_pairs={{1,0},{2,1},{3,2},{4,3},{5,4},{6,5},{7,6},{9,8},{10,9},{11,10},{12... | collective-permute-start | bytes 147464 | tf_op jit(solution)/shard_map/ppermute | solution.py:24
  25.7 1.6 copy-start.20
  26.1 1.3 copy-start.22
  94.8 2.0 copy-start.25
  104.4 2.3 copy-start.7
  104.4 2.3 copy-start.19
  104.4 2.3 copy-start.26
  122.1 1.3 copy-start.1
  147.7 1.3 copy-start.1
  209.6 2.5 copy-start.27
  209.6 2.5 copy-start.6
  209.6 2.5 copy-start.12
  209.6 9.2 %copy-start.4 = (f32[4,416,256]{2,1,0:T(8,128)S(1)}, f32[4,416,256]{2,1,0:T(8,128)}, u32[]{:S(2)}) copy-start(f32[4,416,256]{2,1,0:T(8,128)} %get-tuple-element.221) | copy-start | bytes 5111812
  209.6 9.3 %copy-start.21 = (bf16[4,48,128]{2,1,0:T(8,128)(2,1)S(1)}, bf16[4,48,128]{2,1,0:T(8,128)(2,1)}, u32[]{:S(2)}) copy-start(bf16[4,48,128]{2,1,0:T(8,128)(2,1)} %copy-done.20) | copy-start | bytes 147460
  209.6 9.3 %copy-start.23 = (bf16[4,48,128]{2,1,0:T(8,128)(2,1)S(1)}, bf16[4,48,128]{2,1,0:T(8,128)(2,1)}, u32[]{:S(2)}) copy-start(bf16[4,48,128]{2,1,0:T(8,128)(2,1)} %copy-done.22) | copy-start | bytes 147460
  212.7 7.8 %collective-permute-start.4 = (bf16[4,48,128]{2,1,0:T(8,128)(2,1)S(1)}, bf16[4,48,128]{2,1,0:T(8,128)(2,1)S(1)}, u32[]{:S(2)}, u32[]{:S(2)}) collective-permute-start(bf16[4,48,128]{2,1,0:T(8,128)(2,1)S(1)} %get-tuple-element.302), channel_id=1, source_target_pairs={{0,1},{1,2},{2,3},{3,4},{4,5},{5,6},{6,7},{8,9},{9,10},{10,11},{11... | collective-permute-start | bytes 147464 | tf_op jit(solution)/shard_map/ppermute | solution.py:32
  217.4 3.1 copy-start.28
  217.4 3.8 copy-start.3
  217.4 3.8 copy-start.24
  217.4 3.7 collective-permute-start.5
  221.2 2.8 copy-start.29
  221.2 49.1 %copy-start.8 = (f32[4,320,128]{2,1,0:T(8,128)S(1)}, f32[4,320,128]{2,1,0:T(8,128)}, u32[]{:S(2)}) copy-start(f32[4,320,128]{2,1,0:T(8,128)} %copy-done.7) | copy-start | bytes 1966084
  221.2 49.1 %copy-start.10 = (bf16[4,320,128]{2,1,0:T(8,128)(2,1)S(1)}, bf16[4,320,128]{2,1,0:T(8,128)(2,1)}, u32[]{:S(2)}) copy-start(bf16[4,320,128]{2,1,0:T(8,128)(2,1)} %param.25) | copy-start | bytes 983044
  356.4 15.1 %copy-start.14 = (f32[128,128]{1,0:T(8,128)S(1)}, f32[128,128]{1,0:T(8,128)}, u32[]{:S(2)}) copy-start(f32[128,128]{1,0:T(8,128)} %get-tuple-element.270) | copy-start | bytes 196612
  356.4 15.7 %copy-start.13 = (f32[128,384]{1,0:T(8,128)S(1)}, f32[128,384]{1,0:T(8,128)}, u32[]{:S(2)}) copy-start(f32[128,384]{1,0:T(8,128)} %get-tuple-element.269) | copy-start | bytes 589828
  (14 other events, 14.2 us)
Sparse Core Ops, SparseCore 0:
  220.6 135.7 all-reduce.11
where the time goes:
time: 383 us; the launch traced here: 380 us
  local copies, waits for them, and re-layouts  96.1 us (25%)
  waiting for transfers between devices  85.5 us (22%)
  other arithmetic  71.7 us (19%)
  matrix products  46 us (12%)
  blocking collectives  44.4 us (12%)
  between operations  19 us (5%)
  starting transfers between devices  16.2 us (4%)
    psum x1, waiting for transfers between devices, on_device(): lax.psum((gradients[0], gradients[1], gradients[2], gradients[3], gradien...  84.5 us
    slice x40, local copies, waits for them, and re-layouts, attend(): blocks[offset:offset + window_count]  57.2 us
    psum x1, blocking collectives, on_device(): lax.psum((gradients[0], gradients[1], gradients[2], gradients[3], gradien...  44.4 us
    concatenate x8, other arithmetic, attend(): jnp.concatenate([blocks[offset:offset + window_count] for offset in range...  22.3 us
    dot_general x12, matrix products, attend(): jnp.einsum('whqk,wkhd->wqhd', weights, values_in, precision=PRECISE)  16.2 us
    dot_general x16, matrix products, attend(): jnp.einsum('wqhd,wkhd->whqk', query_blocks, keys_in, precision=PRECISE)  12.1 us
    reduce_sum x7, other arithmetic, on_device(): squares = sum((jnp.sum(member * member) for member in totals))  8.12 us
  transfers between devices with their start and end apart: 7, of which 3 were waited for; matrix products, arithmetic and copies ran while one was open for 4% of the time, Pallas kernels for 0%

commit v1 on v0

--- a/solution.py
+++ b/solution.py
@@ -206,7 +206,10 @@
         grad_transit,
         grad_return,
     )
-    totals = lax.psum(
+    _step_on_steps_all = lambda target: jax.lax.psum(
+        jax.lax.psum(target, axis_name="samp"), axis_name="atom"
+    )
+    totals = _step_on_steps_all(
         (
             gradients[0],
             gradients[1],
@@ -215,8 +218,7 @@
             gradients[4],
             gradients[5],
             gradients[6],
-        ),
-        ("samp", "atom"),
+        )
     )
     squares = sum((jnp.sum(member * member) for member in totals))
     factor = CLIP_NORM / jnp.sqrt(squares + CLIP_NORM * CLIP_NORM)

time: 383 us -> 350 us (0.914)
  blocking collectives: 44.4 us -> 26.5 us
  waiting for transfers between devices: 85.5 us -> 73 us
    psum x1 -> x2, blocking collectives: 44.4 us -> 26.5 us  [the longest x1 14.4 us: on_device(): jax.lax.psum(jax.lax.psum(target, axis_name='samp'), axis_name='atom')]
    psum x1 -> x2, waiting for transfers between devices: 84.5 us -> 72 us  [the longest x1 56.6 us: on_device(): jax.lax.psum(jax.lax.psum(target, axis_name='samp'), axis_name='atom')]
  transfers between devices with their start and end apart: 7 -> 8, of which waited for: 3 -> 4; matrix products, arithmetic and copies ran while one was open for 4% -> 4% of each run, Pallas kernels for 0% -> 0%
where the time goes in v1:
time: 350 us; the launch traced here: 348 us
  local copies, waits for them, and re-layouts  96.1 us (27%)
  waiting for transfers between devices  73 us (21%)
  other arithmetic  71.7 us (20%)
  matrix products  44.4 us (13%)
  blocking collectives  26.5 us (8%)
  between operations  19 us (5%)
  starting transfers between devices  16.3 us (5%)
    slice x40, local copies, waits for them, and re-layouts, attend(): blocks[offset:offset + window_count]  57.2 us
    psum x1, waiting for transfers between devices, on_device(): jax.lax.psum(jax.lax.psum(target, axis_name='samp'), axis_name='atom')  56.6 us
    concatenate x8, other arithmetic, attend(): jnp.concatenate([blocks[offset:offset + window_count] for offset in range...  22.3 us
    dot_general x12, matrix products, attend(): jnp.einsum('whqk,wkhd->wqhd', weights, values_in, precision=PRECISE)  16.2 us
    psum x1, waiting for transfers between devices, on_device(): jax.lax.psum(target, axis_name='samp')  15.4 us
    psum x1, blocking collectives, on_device(): jax.lax.psum(jax.lax.psum(target, axis_name='samp'), axis_name='atom')  14.4 us
    dot_general x16, matrix products, attend(): jnp.einsum('wqhd,wkhd->whqk', query_blocks, keys_in, precision=PRECISE)  12.2 us
    psum x1, blocking collectives, on_device(): jax.lax.psum(target, axis_name='samp')  12.1 us
  transfers between devices with their start and end apart: 8, of which 4 were waited for; matrix products, arithmetic and copies ran while one was open for 4% of the time, Pallas kernels for 0%

profile of v1, /device:TPU:0, one launch (start us, length us, event | category | flops | bytes accessed | tf_op | source)
XLA Modules:
  0.0 348.1 jit_solution(935465914198966)
XLA Ops:
  8.9 2.4 collective-permute-start.2
  16.6 5.1 %collective-permute-start = (bf16[4,48,128]{2,1,0:T(8,128)(2,1)S(1)}, bf16[4,48,128]{2,1,0:T(8,128)(2,1)S(1)}, u32[]{:S(2)}, u32[]{:S(2)}) collective-permute-start(bf16[4,48,128]{2,1,0:T(8,128)(2,1)S(1)} %get-tuple-element.311), channel_id=1, source_target_pairs={{0,1},{1,2},{2,3},{3,4},{4,5},{5,6},{6,7},{8,9},{9,10},{10,11},{11... | collective-permute-start | bytes 147464 | tf_op jit(solution)/shard_map/ppermute | solution.py:23
  27.4 67.5 %while.30 = (s32[]{:T(128)}, bf16[4,320,128]{2,1,0:T(8,128)(2,1)}, bf16[4,416,256]{2,1,0:T(8,128)(2,1)}, s32[10,1,1,128]{3,0,2,1:T(8,128)S(1)}, bf16[4,320,128]{...) while((s32[]{:T(128)}, bf16[4,320,128]{2,1,0:T(8,128)(2,1)}, ...), condition=%wide.region_5.6_spmd.clone, body=%wide.region_2.5_spmd.sunk.clone | while | flops 128473856 | bytes 16410097 | solution.py:125
  33.0 2.4 copy.101
  36.9 2.8 pad_maximum_fusion.13
  49.9 2.4 copy.101
  53.8 2.8 pad_maximum_fusion.13
  66.7 2.4 copy.101
  70.7 2.8 pad_maximum_fusion.13
  83.6 2.4 copy.101
  87.5 2.8 pad_maximum_fusion.13
  106.3 102.9 %while.31 = (s32[]{:T(128)}, f32[4,320,128]{2,1,0:T(8,128)}, f32[4,416,256]{2,1,0:T(8,128)}, f32[4,4]{1,0:T(4,128)S(1)}, s32[10,1,1,128]{3,0,2,1:T(8,128)S(1)}, ...) while((s32[]{:T(128)}, f32[4,320,128]{2,1,0:T(8,128)}, ...), condition=%wide.region_15.16_spmd.clone, body=%wide.region_10.15_spmd.sunk.clone | while | flops 319997184 | bytes 31044328 | solution.py:175
  113.9 2.4 copy.108
  116.3 2.4 copy.109
  118.8 2.8 pad_maximum_fusion.14
  139.6 2.4 copy.108
  142.0 2.4 copy.109
  144.4 2.8 pad_maximum_fusion.14
  165.2 2.4 copy.108
  167.7 2.4 copy.109
  170.1 2.8 pad_maximum_fusion.14
  190.9 2.4 copy.108
  193.4 2.4 copy.109
  195.8 2.8 pad_maximum_fusion.14
  209.2 2.5 fusion.84
  212.3 4.7 %collective-permute-start.4 = (bf16[4,48,128]{2,1,0:T(8,128)(2,1)S(1)}, bf16[4,48,128]{2,1,0:T(8,128)(2,1)S(1)}, u32[]{:S(2)}, u32[]{:S(2)}) collective-permute-start(bf16[4,48,128]{2,1,0:T(8,128)(2,1)S(1)} %get-tuple-element.309), channel_id=1, source_target_pairs={{0,1},{1,2},{2,3},{3,4},{4,5},{5,6},{6,7},{8,9},{9,10},{10,11},{11... | collective-permute-start | bytes 147464 | tf_op jit(solution)/shard_map/ppermute | solution.py:32
  222.3 12.1 %all-reduce.10 = (f32[128]{0:T(128)S(1)}, f32[4]{0:T(128)S(1)}, f32[128]{0:T(128)S(1)}) all-reduce(f32[128]{0:T(128)S(1)} %get-tuple-element.226, f32[4]{0:T(128)S(1)} %reduce_sum.232, f32[128]{0:T(128)S(1)} %get-tuple-element.224), channel_id=1, replica_groups=mesh['samp'=4,'atom'=8] {'samp'}, use_global_device_ids=true, to_apply=%region_19.20 | all-reduce | flops 260 | bytes 2080 | tf_op jit(solution)/shard_map/psum | solution.py:210
  234.5 14.4 %all-reduce.8 = (f32[128]{0:T(128)S(1)}, f32[4]{0:T(128)S(1)}, f32[128]{0:T(128)S(1)}) all-reduce(f32[128]{0:T(128)S(1)} %get-tuple-element.273, f32[4]{0:T(128)S(1)} %get-tuple-element.274, f32[128]{0:T(128)S(1)} %get-tuple-element.275), channel_id=1, replica_groups=mesh['samp'=4,'atom'=8] {'atom'}, use_global_device_ids=true, to_apply=%region_20.21 | all-reduce | flops 260 | bytes 2080 | tf_op jit(solution)/shard_map/psum | solution.py:209
  250.1 15.4 %all-reduce.17.cloned.1.call-done = (f32[128,384]{1,0:T(8,128)}, f32[128,128]{1,0:T(8,128)}, f32[128,512]{1,0:T(8,128)}, f32[256,128]{1,0:T(8,128)}) async-done(((f32[128,384]{1,0:T(8,128)}, f32[128,128]{1,0:T(8,128)}, f32[128,512]{1,0:T(8,128)}, f32[256,128]{1,0:T(8,128)}), (f32[128,384]{1,0:T(8,128)}, f32[128,128]{1,0:T(8,128)}, f32[128,512]{1,0:T(8,128)}, ...) | async-done | bytes 655376 | tf_op jit(solution)/shard_map/psum | solution.py:210
  266.2 1.7 add_convert_fusion
  267.8 56.6 %all-reduce.15.cloned.1.call-done = (f32[128,384]{1,0:T(8,128)}, f32[128,128]{1,0:T(8,128)}, f32[128,512]{1,0:T(8,128)}, f32[256,128]{1,0:T(8,128)}) async-done(((f32[128,384]{1,0:T(8,128)}, f32[128,128]{1,0:T(8,128)}, f32[128,512]{1,0:T(8,128)}, f32[256,128]{1,0:T(8,128)}), (f32[128,384]{1,0:T(8,128)}, f32[128,128]{1,0:T(8,128)}, f32[128,512]{1,0:T(8,128)}, ...) | async-done | bytes 655376 | tf_op jit(solution)/shard_map/psum | solution.py:209
  337.3 1.7 broadcast_multiply_fusion
  (339 shorter events, 160.0 us)
Async XLA Ops:
  7.2 89.7 %copy-start = (bf16[128,512]{1,0:T(8,128)(2,1)S(1)}, bf16[128,512]{1,0:T(8,128)(2,1)}, u32[]{:S(2)}) copy-start(bf16[128,512]{1,0:T(8,128)(2,1)} %param.23) | copy-start | bytes 393220
  7.2 16.6 %copy-start.15 = (bf16[128,384]{1,0:T(8,128)(2,1)S(1)}, bf16[128,384]{1,0:T(8,128)(2,1)}, u32[]{:S(2)}) copy-start(bf16[128,384]{1,0:T(8,128)(2,1)} %param.19) | copy-start | bytes 294916
  7.2 258.3 %all-reduce.17.cloned.1.call-start = ((), (), s32[]{:S(2)}) async-start(), calls=%async_computation.1 | async-start | bytes 1310720 | tf_op jit(solution)/shard_map/psum | solution.py:210
  8.9 15.9 %collective-permute-start.2 = (s32[48]{0:T(128)S(1)}, s32[48]{0:T(128)S(1)}, u32[]{:S(2)}, u32[]{:S(2)}) collective-permute-start(s32[48]{0:T(128)S(1)} %get-tuple-element.317), channel_id=1, source_target_pairs={{0,1},{1,2},{2,3},{3,4},{4,5},{5,6},{6,7},{8,9},{9,10},{10,11},{11... | collective-permute-start | bytes 584 | tf_op jit(solution)/shard_map/ppermute | solution.py:23
  11.3 13.5 %collective-permute-start.3 = (s32[48]{0:T(128)S(1)}, s32[48]{0:T(128)S(1)}, u32[]{:S(2)}, u32[]{:S(2)}) collective-permute-start(s32[48]{0:T(128)S(1)} %get-tuple-element.318), channel_id=1, source_target_pairs={{1,0},{2,1},{3,2},{4,3},{5,4},{6,5},{7,6},{9,8},{10,9},{11,10},{12... | collective-permute-start | bytes 584 | tf_op jit(solution)/shard_map/ppermute | solution.py:24
  16.6 10.8 %copy-start.5 = (bf16[4,320,128]{2,1,0:T(8,128)(2,1)}, bf16[4,320,128]{2,1,0:T(8,128)(2,1)S(1)}, u32[]{:S(2)}) copy-start(bf16[4,320,128]{2,1,0:T(8,128)(2,1)S(1)} %fusion.39) | copy-start | bytes 983044
  16.6 9.1 %collective-permute-start = (bf16[4,48,128]{2,1,0:T(8,128)(2,1)S(1)}, bf16[4,48,128]{2,1,0:T(8,128)(2,1)S(1)}, u32[]{:S(2)}, u32[]{:S(2)}) collective-permute-start(bf16[4,48,128]{2,1,0:T(8,128)(2,1)S(1)} %get-tuple-element.311), channel_id=1, source_target_pairs={{0,1},{1,2},{2,3},{3,4},{4,5},{5,6},{6,7},{8,9},{9,10},{10,11},{11... | collective-permute-start | bytes 147464 | tf_op jit(solution)/shard_map/ppermute | solution.py:23
  21.7 4.4 %collective-permute-start.1 = (bf16[4,48,128]{2,1,0:T(8,128)(2,1)S(1)}, bf16[4,48,128]{2,1,0:T(8,128)(2,1)S(1)}, u32[]{:S(2)}, u32[]{:S(2)}) collective-permute-start(bf16[4,48,128]{2,1,0:T(8,128)(2,1)S(1)} %get-tuple-element.312), channel_id=1, source_target_pairs={{1,0},{2,1},{3,2},{4,3},{5,4},{6,5},{7,6},{9,8},{10,9},{11,10},{12... | collective-permute-start | bytes 147464 | tf_op jit(solution)/shard_map/ppermute | solution.py:24
  25.7 1.6 copy-start.20
  26.1 1.3 copy-start.22
  94.8 2.0 copy-start.25
  104.0 2.3 copy-start.7
  104.0 2.3 copy-start.19
  104.0 2.3 copy-start.26
  121.7 1.3 copy-start.1
  147.3 1.3 copy-start.1
  173.0 1.3 copy-start.1
  198.7 1.3 copy-start.1
  209.2 2.5 copy-start.6
  209.2 2.5 copy-start.12
  209.2 9.2 %copy-start.4 = (f32[4,416,256]{2,1,0:T(8,128)S(1)}, f32[4,416,256]{2,1,0:T(8,128)}, u32[]{:S(2)}) copy-start(f32[4,416,256]{2,1,0:T(8,128)} %get-tuple-element.221) | copy-start | bytes 5111812
  209.2 9.2 %copy-start.21 = (bf16[4,48,128]{2,1,0:T(8,128)(2,1)S(1)}, bf16[4,48,128]{2,1,0:T(8,128)(2,1)}, u32[]{:S(2)}) copy-start(bf16[4,48,128]{2,1,0:T(8,128)(2,1)} %copy-done.20) | copy-start | bytes 147460
  209.2 9.2 %copy-start.23 = (bf16[4,48,128]{2,1,0:T(8,128)(2,1)S(1)}, bf16[4,48,128]{2,1,0:T(8,128)(2,1)}, u32[]{:S(2)}) copy-start(bf16[4,48,128]{2,1,0:T(8,128)(2,1)} %copy-done.22) | copy-start | bytes 147460
  212.3 7.8 %collective-permute-start.4 = (bf16[4,48,128]{2,1,0:T(8,128)(2,1)S(1)}, bf16[4,48,128]{2,1,0:T(8,128)(2,1)S(1)}, u32[]{:S(2)}, u32[]{:S(2)}) collective-permute-start(bf16[4,48,128]{2,1,0:T(8,128)(2,1)S(1)} %get-tuple-element.309), channel_id=1, source_target_pairs={{0,1},{1,2},{2,3},{3,4},{4,5},{5,6},{6,7},{8,9},{9,10},{10,11},{11... | collective-permute-start | bytes 147464 | tf_op jit(solution)/shard_map/ppermute | solution.py:32
  217.0 3.8 %copy-start.3 = (bf16[4,320,128]{2,1,0:T(8,128)(2,1)S(1)}, bf16[4,320,128]{2,1,0:T(8,128)(2,1)}, u32[]{:S(2)}) copy-start(bf16[4,320,128]{2,1,0:T(8,128)(2,1)} %param.15) | copy-start | bytes 983044
  217.0 3.8 %copy-start.24 = (f32[128]{0:T(128)S(1)}, f32[128]{0:T(128)}, u32[]{:S(2)}) copy-start(f32[128]{0:T(128)} %param.18) | copy-start | bytes 1540
  217.0 3.7 %collective-permute-start.5 = (bf16[4,48,128]{2,1,0:T(8,128)(2,1)S(1)}, bf16[4,48,128]{2,1,0:T(8,128)(2,1)S(1)}, u32[]{:S(2)}, u32[]{:S(2)}) collective-permute-start(bf16[4,48,128]{2,1,0:T(8,128)(2,1)S(1)} %get-tuple-element.310), channel_id=1, source_target_pairs={{1,0},{2,1},{3,2},{4,3},{5,4},{6,5},{7,6},{9,8},{10,9},{11,10},{12... | collective-permute-start | bytes 147464 | tf_op jit(solution)/shard_map/ppermute | solution.py:32
  220.1 104.3 %all-reduce.15.cloned.1.call-start = ((), (), s32[]{:S(2)}) async-start(), calls=%async_computation | async-start | bytes 1310720 | tf_op jit(solution)/shard_map/psum | solution.py:209
  221.4 44.8 %copy-start.8 = (f32[4,320,128]{2,1,0:T(8,128)S(1)}, f32[4,320,128]{2,1,0:T(8,128)}, u32[]{:S(2)}) copy-start(f32[4,320,128]{2,1,0:T(8,128)} %copy-done.7) | copy-start | bytes 1966084
  221.4 44.8 %copy-start.10 = (bf16[4,320,128]{2,1,0:T(8,128)(2,1)S(1)}, bf16[4,320,128]{2,1,0:T(8,128)(2,1)}, u32[]{:S(2)}) copy-start(bf16[4,320,128]{2,1,0:T(8,128)(2,1)} %param.25) | copy-start | bytes 983044
  324.4 15.1 %copy-start.14 = (f32[128,128]{1,0:T(8,128)S(1)}, f32[128,128]{1,0:T(8,128)}, u32[]{:S(2)}) copy-start(f32[128,128]{1,0:T(8,128)} %get-tuple-element.270) | copy-start | bytes 196612
  324.4 15.7 %copy-start.13 = (f32[128,384]{1,0:T(8,128)S(1)}, f32[128,384]{1,0:T(8,128)}, u32[]{:S(2)}) copy-start(f32[128,384]{1,0:T(8,128)} %get-tuple-element.269) | copy-start | bytes 589828
  (12 other events, 11.6 us)
Sparse Core Ops, SparseCore 0:
  220.2 45.3 all-reduce.16
  269.0 55.3 all-reduce.14
